TPU v7x, 256 devices: a whole 4x4x8 slice. The times are simulated.
256 devices in a mesh: seq: 16 (over x, y_lo, core), exp: 16 (over y_hi, z).
Axes of the slice: x: 4, y: 4 (y_hi: 2, y_lo: 2; y = y_hi * 2 + y_lo), z: 8, core: 2. Of those that a mesh axis runs over, the one named last changes fastest.
Arguments:
- queries: bfloat16 [8, 4096, 2048], P(None, 'seq', 'exp'), may hold values from -5 to 5
- keys: bfloat16 [8, 4096, 2048], P(None, 'seq', 'exp'), may hold values from -5 to 5
- values: bfloat16 [8, 4096, 2048], P(None, 'seq', 'exp'), may hold values from -170 to 170
- seg_ids: int32 [8, 4096], replicated, may hold values from 0 to 3, as said below
- norm_gain: float32 [2048], replicated, may hold values from 0.25 to 1.75
- router_w: bfloat16 [512, 64], replicated, may hold values from -0.25 to 0.25
- expert_ids: int32 [4096, 8, 4, 2], P(('seq', 'exp')), may hold values from 0 to 63, all different within a row; in each aligned block of 512 rows (0 to 511, 512 to 1023, ..., all dimensions but the last counted through in order) at most 32 rows name the same one
- w_in: bfloat16 [64, 512, 1024], P('exp'), may hold values from -0.25 to 0.25
- w_out: bfloat16 [64, 1024, 512], P('exp'), may hold values from -0.1875 to 0.1875
Outputs:
- normed: bfloat16 [8, 4096, 2048], P(None, ('seq', 'exp'))
- expert_mix: bfloat16 [8, 4096, 2048], P(None, ('seq', 'exp'))
Inputs may be any that keep to these rules, and one draw needn't show every extreme that they name: `seg_ids`: in each sequence the numbers start at 0, never fall, and rise by one at each of 3 document starts; every start lies at an even position after the middle of the sequence. `expert_ids`: the 2 experts of a sub-token differ. Among the rows of one device (its 16 positions, all sequences, all sub-tokens) no expert is named more than 32 times; in every draw some device names some expert exactly 32 times.
All inputs are finite; a program needn't handle non-finite values.
Results may differ from a plain program's by a relative error of at most 0.015.
Values may be sent and summed in bfloat16 or wider, within the bound.
A program may use at most 128 MiB of HBM per device.

v0:
```python
import jax
import jax.numpy as jnp
from jax import lax
from jax.sharding import PartitionSpec as P

HD = 128
SUB = 512
TOPK = 2
CAP = 32
NEG = -1e30


def update(running, query_heads, shaped, query_pos, query_seg, key_pos, key_seg, score_scale):
    maxima, totals, running_total = running
    attention_scores = (
        jnp.einsum("bqhd,bkhd->bhqk", query_heads, shaped[0], preferred_element_type=jnp.float32)
        * score_scale
    )
    visible = (key_pos[None, :] <= query_pos[:, None])[None, None] & (
        key_seg[:, None, None, :] == query_seg[:, None, :, None]
    )
    highest = jnp.max(jnp.where(visible, attention_scores, NEG), axis=-1)
    new_max = jnp.maximum(maxima, highest)
    weights = jnp.where(visible, jnp.exp(attention_scores - new_max[..., None]), 0.0)
    rescale_factor = jnp.exp(maxima - new_max)
    totals = totals * rescale_factor + jnp.sum(weights, axis=-1)
    rounded_result = weights.astype(jnp.bfloat16)
    running_total = running_total * rescale_factor[..., None] + jnp.einsum(
        "bhqk,bkhd->bhqd", rounded_result, shaped[1], preferred_element_type=jnp.float32
    )
    return (new_max, totals, running_total)


def attend_block(
    running, query_heads, block, query_pos, query_seg, seg_ids, key_first, score_scale
):
    row_count = block.shape[2]
    key_pos = key_first + jnp.arange(row_count, dtype=jnp.int32)
    key_seg = lax.dynamic_slice_in_dim(seg_ids, key_first, row_count, 1)
    needed = (key_first <= query_pos[-1]) & jnp.any(key_seg[:, -1] >= query_seg[:, 0])
    shaped = block.reshape(2, block.shape[1], row_count, query_heads.shape[2], query_heads.shape[3])
    return lax.cond(
        needed,
        lambda state: update(
            state, query_heads, shaped, query_pos, query_seg, key_pos, key_seg, score_scale
        ),
        lambda state: state,
        running,
    )


def body(queries, keys, values, seg_ids, norm_gain, router_w, expert_ids, w_in, w_out):
    my_index = lax.axis_index("seq")
    seq_count, local_len, local_width = queries.shape
    head_count = local_width // HD
    score_scale = HD ** (-0.5)
    first_pos = my_index * local_len
    query_pos = first_pos + jnp.arange(local_len, dtype=jnp.int32)
    query_seg = lax.dynamic_slice_in_dim(seg_ids, first_pos, local_len, 1)
    query_heads = queries.reshape(seq_count, local_len, head_count, HD)
    initial = (
        jnp.full((seq_count, head_count, local_len), NEG, jnp.float32),
        jnp.zeros((seq_count, head_count, local_len), jnp.float32),
        jnp.zeros((seq_count, head_count, local_len, HD), jnp.float32),
    )
    stacked = jnp.stack([keys, values])

    def attend(running, block, key_first):
        return attend_block(
            running, query_heads, block, query_pos, query_seg, seg_ids, key_first, score_scale
        )

    shard_part = lax.all_gather(stacked, "seq", axis=2, tiled=True)
    row_count = shard_part.shape[2]
    width = min(row_count, local_len)
    repeats = row_count // width

    def inner(number, state):
        section = lax.dynamic_slice_in_dim(shard_part, number * width, width, 2)
        return attend(state, section, number * width)

    running = lax.fori_loop(0, repeats, inner, initial)
    maxima, totals, running_total = running
    attended = (
        (running_total / totals[..., None])
        .transpose(0, 2, 1, 3)
        .reshape(seq_count, local_len, local_width)
        .astype(jnp.bfloat16)
    )
    tokens = lax.all_to_all(attended, "exp", split_axis=1, concat_axis=2, tiled=True)
    values32 = tokens.astype(jnp.float32)
    spread = jnp.sqrt(jnp.mean(values32 * values32, axis=-1, keepdims=True) + 1e-06)
    normed = (values32 / spread * norm_gain).astype(jnp.bfloat16)
    token_count = normed.shape[1]
    feature_count = normed.shape[2]
    sub_count = feature_count // SUB
    sub_rows = (
        normed.reshape(seq_count, token_count, sub_count, SUB)
        .transpose(1, 0, 2, 3)
        .reshape(-1, SUB)
    )
    picks = expert_ids.reshape(-1, TOPK)
    logits = jnp.dot(sub_rows, router_w, preferred_element_type=jnp.float32)
    chosen = jnp.take_along_axis(logits, picks, axis=1)
    sigmas = jax.nn.sigmoid(chosen)
    gates = sigmas / jnp.sum(sigmas, axis=1, keepdims=True)
    expert_total = router_w.shape[1]
    targets = picks.reshape(-1)
    one_hot = (targets[:, None] == jnp.arange(expert_total, dtype=jnp.int32)[None, :]).astype(
        jnp.int32
    )
    earlier = jnp.cumsum(one_hot, axis=0) - one_hot
    slot_rank = jnp.sum(earlier * one_hot, axis=1)
    destination = targets * CAP + slot_rank
    sources = jnp.arange(targets.shape[0], dtype=jnp.int32) // TOPK
    outgoing = (
        jnp.zeros((expert_total * CAP, SUB), jnp.bfloat16)
        .at[destination]
        .set(sub_rows[sources])
        .reshape(expert_total, CAP, SUB)
    )
    arrived = lax.all_to_all(outgoing, "exp", split_axis=0, concat_axis=1, tiled=True)
    hidden = jax.nn.gelu(
        jnp.einsum("ecs,esf->ecf", arrived, w_in, preferred_element_type=jnp.float32),
        approximate=True,
    ).astype(jnp.bfloat16)
    results = jnp.einsum("ecf,efs->ecs", hidden, w_out, preferred_element_type=jnp.float32).astype(
        jnp.bfloat16
    )
    returned = lax.all_to_all(results, "exp", split_axis=1, concat_axis=0, tiled=True).reshape(
        expert_total * CAP, SUB
    )
    picked = returned[destination].reshape(-1, TOPK, SUB).astype(jnp.float32)
    mixed = jnp.sum(gates[:, :, None] * picked, axis=1).astype(jnp.bfloat16)
    expert_mix = mixed.reshape(token_count, seq_count, feature_count).transpose(1, 0, 2)
    return (normed, expert_mix)


def solution(mesh):
    return jax.shard_map(
        body,
        mesh=mesh,
        in_specs=(
            P(None, "seq", "exp"),
            P(None, "seq", "exp"),
            P(None, "seq", "exp"),
            P(),
            P(),
            P(),
            P(("seq", "exp"), None, None, None),
            P("exp", None, None),
            P("exp", None, None),
        ),
        out_specs=(P(None, ("seq", "exp"), None), P(None, ("seq", "exp"), None)),
        check_vma=False,
    )
```

profile of v0, /device:TPU:7, one launch (start us, length us, event | category | flops | bytes accessed | tf_op | source)
XLA Modules:
  0.0 494.1 jit_solution(5540001684064581826)
XLA Ops:
  12.8 94.3 %all-gather.2.cloned.1.call-done = bf16[2,8,4096,128]{3,2,1,0:T(8,128)(2,1)} async-done(((bf16[2,8,256,128]{3,2,1,0:T(8,128)(2,1)}), bf16[2,8,4096,128]{3,2,1,0:T(8,128)(2,1)}) %all-gather.2.cloned.1.call-update) | async-done | bytes 16777232 | tf_op jit(solution)/shard_map/all_gather | solution.py:73
  107.8 198.1 %while.17 = (s32[]{:T(128)}, f32[8,1,256]{2,0,1:T(8,128)S(1)}, f32[8,1,256]{2,0,1:T(8,128)}, f32[8,1,256,128]{3,2,0,1:T(8,128)S(1)}, s32[256]{0:T(256)}, /*index...) while((s32[]{:T(128)}, f32[8,1,256]{2,0,1:T(8,128)S(1)}, ...), condition=%wide.region_6.7_spmd, body=%wide.region_0.6_spmd.sunk | while | flops 277944608 | bytes 10492413 | solution.py:82
  112.4 8.8 %conditional.2 = ((f32[8,1,256]{2,0,1:T(8,128)S(1)}, f32[8,1,256]{2,0,1:T(8,128)}, f32[8,1,256,128]{3,2,0,1:T(8,128)S(1)})) conditional(s32[]{:T(128)} %convert_element_type.119, (f32[8,1,256]{2,0,1:T(8,128)S(1)}, f32[8,1,256]{2,0,1:T(8,128)}, f32[8,1,256,128]{3,2,0,1:T(8,128)S(1)}) %tuple.51, (s32[]{:T(128)}, s32[256]{0:T(256)S(1)}, s32[256]{0:T(256)}, ...), branch_computations={%region_2.0_spmd, %region_3.5_spmd} | conditional | flops 277944576 | bytes 10474604 | solution.py:42
  115.9 2.4 fusion.5
  125.9 8.8 %conditional.2 = ((f32[8,1,256]{2,0,1:T(8,128)S(1)}, f32[8,1,256]{2,0,1:T(8,128)}, f32[8,1,256,128]{3,2,0,1:T(8,128)S(1)})) conditional(s32[]{:T(128)} %convert_element_type.119, (f32[8,1,256]{2,0,1:T(8,128)S(1)}, f32[8,1,256]{2,0,1:T(8,128)}, f32[8,1,256,128]{3,2,0,1:T(8,128)S(1)}) %tuple.51, (s32[]{:T(128)}, s32[256]{0:T(256)S(1)}, s32[256]{0:T(256)}, ...), branch_computations={%region_2.0_spmd, %region_3.5_spmd} | conditional | flops 277944576 | bytes 10474604 | solution.py:42
  139.4 8.8 %conditional.2 = ((f32[8,1,256]{2,0,1:T(8,128)S(1)}, f32[8,1,256]{2,0,1:T(8,128)}, f32[8,1,256,128]{3,2,0,1:T(8,128)S(1)})) conditional(s32[]{:T(128)} %convert_element_type.119, (f32[8,1,256]{2,0,1:T(8,128)S(1)}, f32[8,1,256]{2,0,1:T(8,128)}, f32[8,1,256,128]{3,2,0,1:T(8,128)S(1)}) %tuple.51, (s32[]{:T(128)}, s32[256]{0:T(256)S(1)}, s32[256]{0:T(256)}, ...), branch_computations={%region_2.0_spmd, %region_3.5_spmd} | conditional | flops 277944576 | bytes 10474604 | solution.py:42
  142.9 2.4 fusion.5
  152.9 8.8 %conditional.2 = ((f32[8,1,256]{2,0,1:T(8,128)S(1)}, f32[8,1,256]{2,0,1:T(8,128)}, f32[8,1,256,128]{3,2,0,1:T(8,128)S(1)})) conditional(s32[]{:T(128)} %convert_element_type.119, (f32[8,1,256]{2,0,1:T(8,128)S(1)}, f32[8,1,256]{2,0,1:T(8,128)}, f32[8,1,256,128]{3,2,0,1:T(8,128)S(1)}) %tuple.51, (s32[]{:T(128)}, s32[256]{0:T(256)S(1)}, s32[256]{0:T(256)}, ...), branch_computations={%region_2.0_spmd, %region_3.5_spmd} | conditional | flops 277944576 | bytes 10474604 | solution.py:42
  156.4 2.4 fusion.5
  166.3 8.8 %conditional.2 = ((f32[8,1,256]{2,0,1:T(8,128)S(1)}, f32[8,1,256]{2,0,1:T(8,128)}, f32[8,1,256,128]{3,2,0,1:T(8,128)S(1)})) conditional(s32[]{:T(128)} %convert_element_type.119, (f32[8,1,256]{2,0,1:T(8,128)S(1)}, f32[8,1,256]{2,0,1:T(8,128)}, f32[8,1,256,128]{3,2,0,1:T(8,128)S(1)}) %tuple.51, (s32[]{:T(128)}, s32[256]{0:T(256)S(1)}, s32[256]{0:T(256)}, ...), branch_computations={%region_2.0_spmd, %region_3.5_spmd} | conditional | flops 277944576 | bytes 10474604 | solution.py:42
  179.8 8.8 %conditional.2 = ((f32[8,1,256]{2,0,1:T(8,128)S(1)}, f32[8,1,256]{2,0,1:T(8,128)}, f32[8,1,256,128]{3,2,0,1:T(8,128)S(1)})) conditional(s32[]{:T(128)} %convert_element_type.119, (f32[8,1,256]{2,0,1:T(8,128)S(1)}, f32[8,1,256]{2,0,1:T(8,128)}, f32[8,1,256,128]{3,2,0,1:T(8,128)S(1)}) %tuple.51, (s32[]{:T(128)}, s32[256]{0:T(256)S(1)}, s32[256]{0:T(256)}, ...), branch_computations={%region_2.0_spmd, %region_3.5_spmd} | conditional | flops 277944576 | bytes 10474604 | solution.py:42
  183.3 2.4 fusion.5
  193.3 8.8 %conditional.2 = ((f32[8,1,256]{2,0,1:T(8,128)S(1)}, f32[8,1,256]{2,0,1:T(8,128)}, f32[8,1,256,128]{3,2,0,1:T(8,128)S(1)})) conditional(s32[]{:T(128)} %convert_element_type.119, (f32[8,1,256]{2,0,1:T(8,128)S(1)}, f32[8,1,256]{2,0,1:T(8,128)}, f32[8,1,256,128]{3,2,0,1:T(8,128)S(1)}) %tuple.51, (s32[]{:T(128)}, s32[256]{0:T(256)S(1)}, s32[256]{0:T(256)}, ...), branch_computations={%region_2.0_spmd, %region_3.5_spmd} | conditional | flops 277944576 | bytes 10474604 | solution.py:42
  206.8 8.8 %conditional.2 = ((f32[8,1,256]{2,0,1:T(8,128)S(1)}, f32[8,1,256]{2,0,1:T(8,128)}, f32[8,1,256,128]{3,2,0,1:T(8,128)S(1)})) conditional(s32[]{:T(128)} %convert_element_type.119, (f32[8,1,256]{2,0,1:T(8,128)S(1)}, f32[8,1,256]{2,0,1:T(8,128)}, f32[8,1,256,128]{3,2,0,1:T(8,128)S(1)}) %tuple.51, (s32[]{:T(128)}, s32[256]{0:T(256)S(1)}, s32[256]{0:T(256)}, ...), branch_computations={%region_2.0_spmd, %region_3.5_spmd} | conditional | flops 277944576 | bytes 10474604 | solution.py:42
  220.2 8.8 %conditional.2 = ((f32[8,1,256]{2,0,1:T(8,128)S(1)}, f32[8,1,256]{2,0,1:T(8,128)}, f32[8,1,256,128]{3,2,0,1:T(8,128)S(1)})) conditional(s32[]{:T(128)} %convert_element_type.119, (f32[8,1,256]{2,0,1:T(8,128)S(1)}, f32[8,1,256]{2,0,1:T(8,128)}, f32[8,1,256,128]{3,2,0,1:T(8,128)S(1)}) %tuple.51, (s32[]{:T(128)}, s32[256]{0:T(256)S(1)}, s32[256]{0:T(256)}, ...), branch_computations={%region_2.0_spmd, %region_3.5_spmd} | conditional | flops 277944576 | bytes 10474604 | solution.py:42
  233.7 8.8 %conditional.2 = ((f32[8,1,256]{2,0,1:T(8,128)S(1)}, f32[8,1,256]{2,0,1:T(8,128)}, f32[8,1,256,128]{3,2,0,1:T(8,128)S(1)})) conditional(s32[]{:T(128)} %convert_element_type.119, (f32[8,1,256]{2,0,1:T(8,128)S(1)}, f32[8,1,256]{2,0,1:T(8,128)}, f32[8,1,256,128]{3,2,0,1:T(8,128)S(1)}) %tuple.51, (s32[]{:T(128)}, s32[256]{0:T(256)S(1)}, s32[256]{0:T(256)}, ...), branch_computations={%region_2.0_spmd, %region_3.5_spmd} | conditional | flops 277944576 | bytes 10474604 | solution.py:42
  237.2 2.4 fusion.5
  247.2 8.8 %conditional.2 = ((f32[8,1,256]{2,0,1:T(8,128)S(1)}, f32[8,1,256]{2,0,1:T(8,128)}, f32[8,1,256,128]{3,2,0,1:T(8,128)S(1)})) conditional(s32[]{:T(128)} %convert_element_type.119, (f32[8,1,256]{2,0,1:T(8,128)S(1)}, f32[8,1,256]{2,0,1:T(8,128)}, f32[8,1,256,128]{3,2,0,1:T(8,128)S(1)}) %tuple.51, (s32[]{:T(128)}, s32[256]{0:T(256)S(1)}, s32[256]{0:T(256)}, ...), branch_computations={%region_2.0_spmd, %region_3.5_spmd} | conditional | flops 277944576 | bytes 10474604 | solution.py:42
  260.7 8.8 %conditional.2 = ((f32[8,1,256]{2,0,1:T(8,128)S(1)}, f32[8,1,256]{2,0,1:T(8,128)}, f32[8,1,256,128]{3,2,0,1:T(8,128)S(1)})) conditional(s32[]{:T(128)} %convert_element_type.119, (f32[8,1,256]{2,0,1:T(8,128)S(1)}, f32[8,1,256]{2,0,1:T(8,128)}, f32[8,1,256,128]{3,2,0,1:T(8,128)S(1)}) %tuple.51, (s32[]{:T(128)}, s32[256]{0:T(256)S(1)}, s32[256]{0:T(256)}, ...), branch_computations={%region_2.0_spmd, %region_3.5_spmd} | conditional | flops 277944576 | bytes 10474604 | solution.py:42
  274.2 8.8 %conditional.2 = ((f32[8,1,256]{2,0,1:T(8,128)S(1)}, f32[8,1,256]{2,0,1:T(8,128)}, f32[8,1,256,128]{3,2,0,1:T(8,128)S(1)})) conditional(s32[]{:T(128)} %convert_element_type.119, (f32[8,1,256]{2,0,1:T(8,128)S(1)}, f32[8,1,256]{2,0,1:T(8,128)}, f32[8,1,256,128]{3,2,0,1:T(8,128)S(1)}) %tuple.51, (s32[]{:T(128)}, s32[256]{0:T(256)S(1)}, s32[256]{0:T(256)}, ...), branch_computations={%region_2.0_spmd, %region_3.5_spmd} | conditional | flops 277944576 | bytes 10474604 | solution.py:42
  287.6 8.8 %conditional.2 = ((f32[8,1,256]{2,0,1:T(8,128)S(1)}, f32[8,1,256]{2,0,1:T(8,128)}, f32[8,1,256,128]{3,2,0,1:T(8,128)S(1)})) conditional(s32[]{:T(128)} %convert_element_type.119, (f32[8,1,256]{2,0,1:T(8,128)S(1)}, f32[8,1,256]{2,0,1:T(8,128)}, f32[8,1,256,128]{3,2,0,1:T(8,128)S(1)}) %tuple.51, (s32[]{:T(128)}, s32[256]{0:T(256)S(1)}, s32[256]{0:T(256)}, ...), branch_computations={%region_2.0_spmd, %region_3.5_spmd} | conditional | flops 277944576 | bytes 10474604 | solution.py:42
  308.3 9.0 %all-to-all-start = ((bf16[8,256,128]{2,0,1:T(8,128)(2,1)}), bf16[8,256,128]{2,0,1:T(8,128)(2,1)S(1)}, u32[]{:S(2)}, u32[]{:S(2)}) async-start(bf16[8,256,128]{2,0,1:T(8,128)(2,1)} %fusion.38), calls=%async_computation | async-start | bytes 1048576 | tf_op jit(solution)/shard_map/all_to_all | solution.py:90
  317.6 18.0 %reduce-window.6 = s32[64,8,128]{2,1,0:T(8,128)S(1)} reduce-window(s32[64,8,128]{2,1,0:T(8,128)S(1)} %copy-done.2, s32[]{:T(128)} %constant.101.clone.1), window={size=1x1x128 pad=0_0x0_0x127_0}, to_apply=%region_10.11 | reduce-window | flops 8323072 | bytes 524292 | tf_op jit(solution)/shard_map/reduce-window
  341.8 13.1 %scatter_custom_fusion = bf16[2048,512]{1,0:T(8,128)(2,1)S(1)} fusion(s32[1024]{0:T(1024)S(1)} %bitcast.122, bf16[512,512]{1,0:T(8,128)(2,1)} %reshape.305, s32[1024]{0:T(1024)S(1)} %broadcast_clamp_fusion.1, bf16[]{:T(256)} %constant.114.clone.1), kind=kCustom, calls=%fused_computation.52 | custom fusion | bytes 2097664 | tf_op jit(solution)/shard_map/scatter | solution.py:119
  354.9 52.7 %all_to_all.42 = bf16[64,32,512]{2,1,0:T(8,128)(2,1)S(1)} all-to-all(bf16[64,32,512]{2,1,0:T(8,128)(2,1)S(1)} %bitcast.110), channel_id=1, replica_groups=mesh['seq'=16,'exp'=16] {'exp'}, dimensions={0} | all-to-all | bytes 4194304 | tf_op jit(solution)/shard_map/all_to_all | solution.py:122
  407.9 9.7 %fusion.31 = bf16[4,512,512]{2,1,0:T(8,128)(2,1)} fusion(bf16[4,1024,512]{2,1,0:T(8,128)(2,1)} %param.21, bf16[4,512,512]{2,1,0:T(8,128)(2,1)S(1)} %bitcast.114, bf16[4,512,1024]{2,1,0:T(8,128)(2,1)} %param.20), kind=kOutput, calls=%fused_computation.48 | convolution fusion | flops 4314890240 | bytes 12582912 | tf_op jit(solution)/shard_map/ecf,efs->ecs/dot_general | solution.py:127
  417.6 4.6 copy.159
  422.2 4.5 all-to-all-start.2
  428.8 8.6 %gather_fusion.1 = f32[1024]{0:T(1024)S(1)} fusion(f32[512,64]{0,1:T(8,128)S(1)} %fusion.54, s32[1024]{0:T(1024)S(1)} %reshape.331), kind=kCustom, calls=%fused_computation.2 | custom fusion | bytes 16384 | tf_op jit(solution)/shard_map/jit(take_along_axis)/gather | solution.py:104
  444.5 29.3 %all-to-all-done.2 = bf16[4,512,512]{2,0,1:T(4,128)(2,1)S(1)} async-done(((bf16[4,512,512]{2,0,1:T(4,128)(2,1)}), bf16[4,512,512]{2,0,1:T(4,128)(2,1)S(1)}, u32[]{:S(2)}, u32[]{:S(2)}) %all-to-all-start.2) | async-done | bytes 2097184 | tf_op jit(solution)/shard_map/all_to_all | solution.py:130
  477.3 4.0 gather_fusion
  482.6 3.2 multiply_reduce_fusion
  (306 shorter events, 195.3 us)
Async XLA Ops:
  7.2 420.3 %copy-start = (bf16[512,64]{0,1:T(8,128)(2,1)S(1)}, bf16[512,64]{0,1:T(8,128)(2,1)}, u32[]{:S(2)}) copy-start(bf16[512,64]{0,1:T(8,128)(2,1)} %param.18) | copy-start | bytes 196612
  7.2 99.9 %all-gather.2.cloned.1.call-start = ((), (), s32[]{:S(2)}) async-start(), calls=%async_computation.3 | async-start | bytes 17825792 | tf_op jit(solution)/shard_map/all_gather | solution.py:73
  112.5 2.9 copy-start.3
  115.9 2.4 copy-start.4
  125.9 2.9 copy-start.3
  129.4 2.4 copy-start.4
  139.4 2.9 copy-start.3
  142.9 2.4 copy-start.4
  152.9 2.9 copy-start.3
  156.4 2.4 copy-start.4
  166.3 2.9 copy-start.3
  169.9 2.4 copy-start.4
  179.8 2.9 copy-start.3
  183.3 2.4 copy-start.4
  193.3 2.9 copy-start.3
  206.8 2.9 copy-start.3
  210.3 2.4 copy-start.4
  220.3 2.9 copy-start.3
  233.8 2.9 copy-start.3
  237.2 2.4 copy-start.4
  247.2 2.9 copy-start.3
  250.7 2.4 copy-start.4
  260.7 2.9 copy-start.3
  274.2 2.9 copy-start.3
  277.7 2.4 copy-start.4
  287.7 2.9 copy-start.3
  305.9 11.4 %copy-start.6 = (s32[16,8,4,2]{0,3,2,1:T(2,128)S(1)}, s32[16,8,4,2]{0,3,2,1:T(2,128)}, u32[]{:S(2)}) copy-start(s32[16,8,4,2]{0,3,2,1:T(2,128)} %param.19) | copy-start | bytes 12292
  305.9 11.7 %copy-start.8 = (f32[2048]{0:T(1024)S(1)}, f32[2048]{0:T(1024)}, u32[]{:S(2)}) copy-start(f32[2048]{0:T(1024)} %param.17) | copy-start | bytes 24580
  305.9 11.7 %copy-start.2 = (s32[64,8,128]{2,1,0:T(8,128)S(1)}, s32[64,8,128]{2,1,0:T(8,128)}, u32[]{:S(2)}) copy-start(s32[64,8,128]{2,1,0:T(8,128)} %fusion.43) | copy-start | bytes 786436
  308.3 28.6 %all-to-all-start = ((bf16[8,256,128]{2,0,1:T(8,128)(2,1)}), bf16[8,256,128]{2,0,1:T(8,128)(2,1)S(1)}, u32[]{:S(2)}, u32[]{:S(2)}) async-start(bf16[8,256,128]{2,0,1:T(8,128)(2,1)} %fusion.38), calls=%async_computation | async-start | bytes 1048576 | tf_op jit(solution)/shard_map/all_to_all | solution.py:90
  422.2 4.5 copy-start.7
  422.2 51.6 %all-to-all-start.2 = ((bf16[4,512,512]{2,0,1:T(4,128)(2,1)}), bf16[4,512,512]{2,0,1:T(4,128)(2,1)S(1)}, u32[]{:S(2)}, u32[]{:S(2)}) async-start(bf16[4,512,512]{2,0,1:T(4,128)(2,1)} %copy.159), calls=%async_computation.2 | async-start | bytes 4194304 | tf_op jit(solution)/shard_map/all_to_all | solution.py:130
  (6 other events, 13.5 us)
Sparse Core Ops, SparseCore 0:
  9.8 97.2 all-gather.1
where the time goes:
time: 499 us; the launch traced here: 494 us
  waiting for transfers between devices  124 us (25%)
  other arithmetic  110 us (22%)
  local copies, waits for them, and re-layouts  84.8 us (17%)
  matrix products  73.9 us (15%)
  blocking collectives  52.7 us (11%)
  loops' own time  21.3 us (4%)
  between operations  14.4 us (3%)
  starting transfers between devices  13.5 us (3%)
    all_gather x1, waiting for transfers between devices, body(): shard_part = lax.all_gather(stacked, 'seq', axis=2, tiled=True)  94.3 us
    all_to_all x1, blocking collectives, body(): lax.all_to_all(outgoing, 'exp', split_axis=0, concat_axis=1, tiled=True)  52.7 us
    dot_general x14, matrix products, update(): jnp.einsum('bhqk,bkhd->bhqd', rounded_result, shaped[1], preferred_elemen...  34 us
    all_to_all x1, waiting for transfers between devices, body(): lax.all_to_all(results, 'exp', split_axis=1, concat_axis=0, tiled=True)  29.3 us
    dot_general x14, matrix products, update(): jnp.einsum('bqhd,bkhd->bhqk', query_heads, shaped[0], preferred_element_t...  28.9 us
    reduce_or x16, other arithmetic, attend_block(): jnp.any(key_seg[:, -1] >= query_seg[:, 0])  22.3 us
    slice x16, local copies, waits for them, and re-layouts, attend_block(): query_pos[-1]  21.3 us
    reduce_sum x14, other arithmetic, update(): totals = totals * rescale_factor + jnp.sum(weights, axis=-1)  21.2 us
  transfers between devices with their start and end apart: 3, of which 2 were waited for; matrix products, arithmetic and copies ran while one was open for 8% of the time, Pallas kernels for 0%

commit v1 on v0

--- a/solution.py
+++ b/solution.py
@@ -70,7 +70,13 @@
             running, query_heads, block, query_pos, query_seg, seg_ids, key_first, score_scale
         )
 
-    shard_part = lax.all_gather(stacked, "seq", axis=2, tiled=True)
+    def save_the_weights(sheet, ax_name):
+        piece_out = tuple((sheet for _ in range(lax.psum(1, axis_name=ax_name))))
+        state_next = jnp.stack(piece_out)
+        x_next = lax.all_to_all(state_next, axis_name=ax_name, split_axis=0, concat_axis=0)
+        return jnp.concatenate(x_next, axis=2)
+
+    shard_part = save_the_weights(stacked, "seq")
     row_count = shard_part.shape[2]
     width = min(row_count, local_len)
     repeats = row_count // width

time: 499 us -> 681 us (1.36)
  waiting for transfers between devices: 124 us -> 291 us
  local copies, waits for them, and re-layouts: 84.8 us -> 105 us
  between operations: 14.4 us -> 1.02 us
  starting transfers between devices: 13.5 us -> 20.4 us
    all_to_all x0 -> x1, waiting for transfers between devices: none -> 260 us  [save_the_weights(): lax.all_to_all(state_next, axis_name=ax_name, split_axis=0, concat_axis=0)]
    all_gather x1 -> x0, waiting for transfers between devices: 94.3 us -> none  [body(): shard_part = lax.all_gather(stacked, 'seq', axis=2, tiled=True)]
    all_to_all x0 -> x1, local copies, waits for them, and re-layouts: none -> 14 us  [save_the_weights(): lax.all_to_all(state_next, axis_name=ax_name, split_axis=0, concat_axis=0)]
    all_to_all x0 -> x1, starting transfers between devices: none -> 7.57 us  [save_the_weights(): lax.all_to_all(state_next, axis_name=ax_name, split_axis=0, concat_axis=0)]
  transfers between devices with their start and end apart: 3 -> 3, of which waited for: 2 -> 2; matrix products, arithmetic and copies ran while one was open for 8% -> 6% of each run, Pallas kernels for 0% -> 0%
where the time goes in v1:
time: 681 us; the launch traced here: 676 us
  waiting for transfers between devices  291 us (43%)
  other arithmetic  109 us (16%)
  local copies, waits for them, and re-layouts  105 us (15%)
  matrix products  74 us (11%)
  blocking collectives  54.2 us (8%)
  loops' own time  21.3 us (3%)
  starting transfers between devices  20.4 us (3%)
    all_to_all x1, waiting for transfers between devices, save_the_weights(): lax.all_to_all(state_next, axis_name=ax_name, split_axis=0, concat_axis=0)  260 us
    all_to_all x1, blocking collectives, body(): lax.all_to_all(outgoing, 'exp', split_axis=0, concat_axis=1, tiled=True)  54.2 us
    dot_general x14, matrix products, update(): jnp.einsum('bhqk,bkhd->bhqd', rounded_result, shaped[1], preferred_elemen...  34 us
    all_to_all x1, waiting for transfers between devices, body(): lax.all_to_all(results, 'exp', split_axis=1, concat_axis=0, tiled=True)  30.8 us
    dot_general x14, matrix products, update(): jnp.einsum('bqhd,bkhd->bhqk', query_heads, shaped[0], preferred_element_t...  29 us
    reduce_or x16, other arithmetic, attend_block(): jnp.any(key_seg[:, -1] >= query_seg[:, 0])  22.4 us
    reduce_sum x14, other arithmetic, update(): totals = totals * rescale_factor + jnp.sum(weights, axis=-1)  21.2 us
    slice x16, local copies, waits for them, and re-layouts, attend_block(): query_pos[-1]  21.2 us
  transfers between devices with their start and end apart: 3, of which 2 were waited for; matrix products, arithmetic and copies ran while one was open for 6% of the time, Pallas kernels for 0%

profile of v1, /device:TPU:7, one launch (start us, length us, event | category | flops | bytes accessed | tf_op | source)
XLA Modules:
  0.0 675.9 jit_solution(15283057003701386479)
XLA Ops:
  2.0 6.2 stack.11
  8.2 7.6 %all-to-all-start = ((bf16[16,2,8,256,128]{4,3,2,1,0:T(8,128)(2,1)}), bf16[16,2,8,256,128]{4,3,2,1,0:T(8,128)(2,1)}, u32[]{:S(2)}, u32[]{:S(2)}) async-start(bf16[16,2,8,256,128]{4,3,2,1,0:T(8,128)(2,1)} %stack.11), calls=%async_computation | async-start | bytes 33554432 | tf_op jit(solution)/shard_map/all_to_all | solution.py:76
  19.0 260.3 %all-to-all-done = bf16[16,2,8,256,128]{4,3,2,1,0:T(8,128)(2,1)} async-done(((bf16[16,2,8,256,128]{4,3,2,1,0:T(8,128)(2,1)}), bf16[16,2,8,256,128]{4,3,2,1,0:T(8,128)(2,1)}, u32[]{:S(2)}, u32[]{:S(2)}) %all-to-all-start) | async-done | bytes 16777248 | tf_op jit(solution)/shard_map/all_to_all | solution.py:76
  279.3 14.0 %copy.167 = bf16[16,2,8,256,128]{4,3,0,2,1:T(8,128)(2,1)} copy(bf16[16,2,8,256,128]{4,3,2,1,0:T(8,128)(2,1)} %all-to-all-done) | data formatting | bytes 33554432 | tf_op jit(solution)/shard_map/all_to_all | solution.py:76
  294.0 198.1 %while.17 = (s32[]{:T(128)}, f32[8,1,256]{2,0,1:T(8,128)S(1)}, f32[8,1,256]{2,0,1:T(8,128)}, f32[8,1,256,128]{3,2,0,1:T(8,128)S(1)}, s32[256]{0:T(256)}, /*index...) while((s32[]{:T(128)}, f32[8,1,256]{2,0,1:T(8,128)S(1)}, ...), condition=%wide.region_6.7_spmd, body=%wide.region_0.6_spmd.sunk | while | flops 277944608 | bytes 10492413 | solution.py:88
  298.7 8.8 %conditional.2 = ((f32[8,1,256]{2,0,1:T(8,128)S(1)}, f32[8,1,256]{2,0,1:T(8,128)}, f32[8,1,256,128]{3,2,0,1:T(8,128)S(1)})) conditional(s32[]{:T(128)} %convert_element_type.119, (f32[8,1,256]{2,0,1:T(8,128)S(1)}, f32[8,1,256]{2,0,1:T(8,128)}, f32[8,1,256,128]{3,2,0,1:T(8,128)S(1)}) %tuple.52, (s32[]{:T(128)}, s32[256]{0:T(256)S(1)}, s32[256]{0:T(256)}, ...), branch_computations={%region_2.0_spmd, %region_3.5_spmd} | conditional | flops 277944576 | bytes 10474604 | solution.py:42
  312.2 8.8 %conditional.2 = ((f32[8,1,256]{2,0,1:T(8,128)S(1)}, f32[8,1,256]{2,0,1:T(8,128)}, f32[8,1,256,128]{3,2,0,1:T(8,128)S(1)})) conditional(s32[]{:T(128)} %convert_element_type.119, (f32[8,1,256]{2,0,1:T(8,128)S(1)}, f32[8,1,256]{2,0,1:T(8,128)}, f32[8,1,256,128]{3,2,0,1:T(8,128)S(1)}) %tuple.52, (s32[]{:T(128)}, s32[256]{0:T(256)S(1)}, s32[256]{0:T(256)}, ...), branch_computations={%region_2.0_spmd, %region_3.5_spmd} | conditional | flops 277944576 | bytes 10474604 | solution.py:42
  315.7 2.4 fusion.5
  325.6 8.8 %conditional.2 = ((f32[8,1,256]{2,0,1:T(8,128)S(1)}, f32[8,1,256]{2,0,1:T(8,128)}, f32[8,1,256,128]{3,2,0,1:T(8,128)S(1)})) conditional(s32[]{:T(128)} %convert_element_type.119, (f32[8,1,256]{2,0,1:T(8,128)S(1)}, f32[8,1,256]{2,0,1:T(8,128)}, f32[8,1,256,128]{3,2,0,1:T(8,128)S(1)}) %tuple.52, (s32[]{:T(128)}, s32[256]{0:T(256)S(1)}, s32[256]{0:T(256)}, ...), branch_computations={%region_2.0_spmd, %region_3.5_spmd} | conditional | flops 277944576 | bytes 10474604 | solution.py:42
  329.2 2.4 fusion.5
  339.1 8.8 %conditional.2 = ((f32[8,1,256]{2,0,1:T(8,128)S(1)}, f32[8,1,256]{2,0,1:T(8,128)}, f32[8,1,256,128]{3,2,0,1:T(8,128)S(1)})) conditional(s32[]{:T(128)} %convert_element_type.119, (f32[8,1,256]{2,0,1:T(8,128)S(1)}, f32[8,1,256]{2,0,1:T(8,128)}, f32[8,1,256,128]{3,2,0,1:T(8,128)S(1)}) %tuple.52, (s32[]{:T(128)}, s32[256]{0:T(256)S(1)}, s32[256]{0:T(256)}, ...), branch_computations={%region_2.0_spmd, %region_3.5_spmd} | conditional | flops 277944576 | bytes 10474604 | solution.py:42
  352.6 8.8 %conditional.2 = ((f32[8,1,256]{2,0,1:T(8,128)S(1)}, f32[8,1,256]{2,0,1:T(8,128)}, f32[8,1,256,128]{3,2,0,1:T(8,128)S(1)})) conditional(s32[]{:T(128)} %convert_element_type.119, (f32[8,1,256]{2,0,1:T(8,128)S(1)}, f32[8,1,256]{2,0,1:T(8,128)}, f32[8,1,256,128]{3,2,0,1:T(8,128)S(1)}) %tuple.52, (s32[]{:T(128)}, s32[256]{0:T(256)S(1)}, s32[256]{0:T(256)}, ...), branch_computations={%region_2.0_spmd, %region_3.5_spmd} | conditional | flops 277944576 | bytes 10474604 | solution.py:42
  366.1 8.8 %conditional.2 = ((f32[8,1,256]{2,0,1:T(8,128)S(1)}, f32[8,1,256]{2,0,1:T(8,128)}, f32[8,1,256,128]{3,2,0,1:T(8,128)S(1)})) conditional(s32[]{:T(128)} %convert_element_type.119, (f32[8,1,256]{2,0,1:T(8,128)S(1)}, f32[8,1,256]{2,0,1:T(8,128)}, f32[8,1,256,128]{3,2,0,1:T(8,128)S(1)}) %tuple.52, (s32[]{:T(128)}, s32[256]{0:T(256)S(1)}, s32[256]{0:T(256)}, ...), branch_computations={%region_2.0_spmd, %region_3.5_spmd} | conditional | flops 277944576 | bytes 10474604 | solution.py:42
  379.5 8.8 %conditional.2 = ((f32[8,1,256]{2,0,1:T(8,128)S(1)}, f32[8,1,256]{2,0,1:T(8,128)}, f32[8,1,256,128]{3,2,0,1:T(8,128)S(1)})) conditional(s32[]{:T(128)} %convert_element_type.119, (f32[8,1,256]{2,0,1:T(8,128)S(1)}, f32[8,1,256]{2,0,1:T(8,128)}, f32[8,1,256,128]{3,2,0,1:T(8,128)S(1)}) %tuple.52, (s32[]{:T(128)}, s32[256]{0:T(256)S(1)}, s32[256]{0:T(256)}, ...), branch_computations={%region_2.0_spmd, %region_3.5_spmd} | conditional | flops 277944576 | bytes 10474604 | solution.py:42
  393.0 8.8 %conditional.2 = ((f32[8,1,256]{2,0,1:T(8,128)S(1)}, f32[8,1,256]{2,0,1:T(8,128)}, f32[8,1,256,128]{3,2,0,1:T(8,128)S(1)})) conditional(s32[]{:T(128)} %convert_element_type.119, (f32[8,1,256]{2,0,1:T(8,128)S(1)}, f32[8,1,256]{2,0,1:T(8,128)}, f32[8,1,256,128]{3,2,0,1:T(8,128)S(1)}) %tuple.52, (s32[]{:T(128)}, s32[256]{0:T(256)S(1)}, s32[256]{0:T(256)}, ...), branch_computations={%region_2.0_spmd, %region_3.5_spmd} | conditional | flops 277944576 | bytes 10474604 | solution.py:42
  406.5 8.8 %conditional.2 = ((f32[8,1,256]{2,0,1:T(8,128)S(1)}, f32[8,1,256]{2,0,1:T(8,128)}, f32[8,1,256,128]{3,2,0,1:T(8,128)S(1)})) conditional(s32[]{:T(128)} %convert_element_type.119, (f32[8,1,256]{2,0,1:T(8,128)S(1)}, f32[8,1,256]{2,0,1:T(8,128)}, f32[8,1,256,128]{3,2,0,1:T(8,128)S(1)}) %tuple.52, (s32[]{:T(128)}, s32[256]{0:T(256)S(1)}, s32[256]{0:T(256)}, ...), branch_computations={%region_2.0_spmd, %region_3.5_spmd} | conditional | flops 277944576 | bytes 10474604 | solution.py:42
  420.0 8.8 %conditional.2 = ((f32[8,1,256]{2,0,1:T(8,128)S(1)}, f32[8,1,256]{2,0,1:T(8,128)}, f32[8,1,256,128]{3,2,0,1:T(8,128)S(1)})) conditional(s32[]{:T(128)} %convert_element_type.119, (f32[8,1,256]{2,0,1:T(8,128)S(1)}, f32[8,1,256]{2,0,1:T(8,128)}, f32[8,1,256,128]{3,2,0,1:T(8,128)S(1)}) %tuple.52, (s32[]{:T(128)}, s32[256]{0:T(256)S(1)}, s32[256]{0:T(256)}, ...), branch_computations={%region_2.0_spmd, %region_3.5_spmd} | conditional | flops 277944576 | bytes 10474604 | solution.py:42
  433.4 8.8 %conditional.2 = ((f32[8,1,256]{2,0,1:T(8,128)S(1)}, f32[8,1,256]{2,0,1:T(8,128)}, f32[8,1,256,128]{3,2,0,1:T(8,128)S(1)})) conditional(s32[]{:T(128)} %convert_element_type.119, (f32[8,1,256]{2,0,1:T(8,128)S(1)}, f32[8,1,256]{2,0,1:T(8,128)}, f32[8,1,256,128]{3,2,0,1:T(8,128)S(1)}) %tuple.52, (s32[]{:T(128)}, s32[256]{0:T(256)S(1)}, s32[256]{0:T(256)}, ...), branch_computations={%region_2.0_spmd, %region_3.5_spmd} | conditional | flops 277944576 | bytes 10474604 | solution.py:42
  446.9 8.8 %conditional.2 = ((f32[8,1,256]{2,0,1:T(8,128)S(1)}, f32[8,1,256]{2,0,1:T(8,128)}, f32[8,1,256,128]{3,2,0,1:T(8,128)S(1)})) conditional(s32[]{:T(128)} %convert_element_type.119, (f32[8,1,256]{2,0,1:T(8,128)S(1)}, f32[8,1,256]{2,0,1:T(8,128)}, f32[8,1,256,128]{3,2,0,1:T(8,128)S(1)}) %tuple.52, (s32[]{:T(128)}, s32[256]{0:T(256)S(1)}, s32[256]{0:T(256)}, ...), branch_computations={%region_2.0_spmd, %region_3.5_spmd} | conditional | flops 277944576 | bytes 10474604 | solution.py:42
  460.4 8.8 %conditional.2 = ((f32[8,1,256]{2,0,1:T(8,128)S(1)}, f32[8,1,256]{2,0,1:T(8,128)}, f32[8,1,256,128]{3,2,0,1:T(8,128)S(1)})) conditional(s32[]{:T(128)} %convert_element_type.119, (f32[8,1,256]{2,0,1:T(8,128)S(1)}, f32[8,1,256]{2,0,1:T(8,128)}, f32[8,1,256,128]{3,2,0,1:T(8,128)S(1)}) %tuple.52, (s32[]{:T(128)}, s32[256]{0:T(256)S(1)}, s32[256]{0:T(256)}, ...), branch_computations={%region_2.0_spmd, %region_3.5_spmd} | conditional | flops 277944576 | bytes 10474604 | solution.py:42
  473.9 8.8 %conditional.2 = ((f32[8,1,256]{2,0,1:T(8,128)S(1)}, f32[8,1,256]{2,0,1:T(8,128)}, f32[8,1,256,128]{3,2,0,1:T(8,128)S(1)})) conditional(s32[]{:T(128)} %convert_element_type.119, (f32[8,1,256]{2,0,1:T(8,128)S(1)}, f32[8,1,256]{2,0,1:T(8,128)}, f32[8,1,256,128]{3,2,0,1:T(8,128)S(1)}) %tuple.52, (s32[]{:T(128)}, s32[256]{0:T(256)S(1)}, s32[256]{0:T(256)}, ...), branch_computations={%region_2.0_spmd, %region_3.5_spmd} | conditional | flops 277944576 | bytes 10474604 | solution.py:42
  494.5 8.4 %all-to-all-start.1 = ((bf16[8,256,128]{2,0,1:T(8,128)(2,1)}), bf16[8,256,128]{2,0,1:T(8,128)(2,1)S(1)}, u32[]{:S(2)}, u32[]{:S(2)}) async-start(bf16[8,256,128]{2,0,1:T(8,128)(2,1)} %fusion.38), calls=%async_computation.1 | async-start | bytes 1048576 | tf_op jit(solution)/shard_map/all_to_all | solution.py:96
  503.2 18.0 %reduce-window.6 = s32[64,8,128]{2,1,0:T(8,128)S(1)} reduce-window(s32[64,8,128]{2,1,0:T(8,128)S(1)} %copy-done.3, s32[]{:T(128)} %constant.101.clone.1), window={size=1x1x128 pad=0_0x0_0x127_0}, to_apply=%region_10.11 | reduce-window | flops 8323072 | bytes 524292 | tf_op jit(solution)/shard_map/reduce-window
  527.4 13.1 %scatter_custom_fusion = bf16[2048,512]{1,0:T(8,128)(2,1)S(1)} fusion(s32[1024]{0:T(1024)S(1)} %bitcast.126, bf16[512,512]{1,0:T(8,128)(2,1)} %reshape.315, s32[1024]{0:T(1024)S(1)} %broadcast_clamp_fusion.1, bf16[]{:T(256)} %constant.114.clone.1), kind=kCustom, calls=%fused_computation.52 | custom fusion | bytes 2097664 | tf_op jit(solution)/shard_map/scatter | solution.py:125
  540.5 54.2 %all_to_all.47 = bf16[64,32,512]{2,1,0:T(8,128)(2,1)S(1)} all-to-all(bf16[64,32,512]{2,1,0:T(8,128)(2,1)S(1)} %bitcast.114), channel_id=1, replica_groups=mesh['seq'=16,'exp'=16] {'exp'}, dimensions={0} | all-to-all | bytes 4194304 | tf_op jit(solution)/shard_map/all_to_all | solution.py:128
  594.9 9.7 %fusion.31 = bf16[4,512,512]{2,1,0:T(8,128)(2,1)} fusion(bf16[4,1024,512]{2,1,0:T(8,128)(2,1)} %param.21, bf16[4,512,512]{2,1,0:T(8,128)(2,1)S(1)} %bitcast.118, bf16[4,512,1024]{2,1,0:T(8,128)(2,1)} %param.20), kind=kOutput, calls=%fused_computation.48 | convolution fusion | flops 4314890240 | bytes 12582912 | tf_op jit(solution)/shard_map/ecf,efs->ecs/dot_general | solution.py:133
  604.7 4.6 copy.189
  609.2 4.5 all-to-all-start.3
  615.9 8.6 %gather_fusion.1 = f32[1024]{0:T(1024)S(1)} fusion(f32[512,64]{0,1:T(8,128)S(1)} %fusion.54, s32[1024]{0:T(1024)S(1)} %reshape.341), kind=kCustom, calls=%fused_computation.2 | custom fusion | bytes 16384 | tf_op jit(solution)/shard_map/jit(take_along_axis)/gather | solution.py:110
  631.6 30.8 %all-to-all-done.3 = bf16[4,512,512]{2,0,1:T(4,128)(2,1)S(1)} async-done(((bf16[4,512,512]{2,0,1:T(4,128)(2,1)}), bf16[4,512,512]{2,0,1:T(4,128)(2,1)S(1)}, u32[]{:S(2)}, u32[]{:S(2)}) %all-to-all-start.3) | async-done | bytes 2097184 | tf_op jit(solution)/shard_map/all_to_all | solution.py:136
  665.9 4.0 gather_fusion
  671.2 3.2 multiply_reduce_fusion
  (309 shorter events, 201.5 us)
Async XLA Ops:
  0.6 613.9 %copy-start = (bf16[512,64]{0,1:T(8,128)(2,1)S(1)}, bf16[512,64]{0,1:T(8,128)(2,1)}, u32[]{:S(2)}) copy-start(bf16[512,64]{0,1:T(8,128)(2,1)} %param.18) | copy-start | bytes 196612
  8.2 7.6 %copy-start.6 = (s32[16,8,4,2]{0,3,2,1:T(2,128)S(1)}, s32[16,8,4,2]{0,3,2,1:T(2,128)}, u32[]{:S(2)}) copy-start(s32[16,8,4,2]{0,3,2,1:T(2,128)} %param.19) | copy-start | bytes 12292
  8.2 271.1 %all-to-all-start = ((bf16[16,2,8,256,128]{4,3,2,1,0:T(8,128)(2,1)}), bf16[16,2,8,256,128]{4,3,2,1,0:T(8,128)(2,1)}, u32[]{:S(2)}, u32[]{:S(2)}) async-start(bf16[16,2,8,256,128]{4,3,2,1,0:T(8,128)(2,1)} %stack.11), calls=%async_computation | async-start | bytes 33554432 | tf_op jit(solution)/shard_map/all_to_all | solution.py:76
  298.7 2.9 copy-start.4
  312.2 2.9 copy-start.4
  315.7 2.4 copy-start.5
  325.7 2.9 copy-start.4
  329.2 2.4 copy-start.5
  339.2 2.9 copy-start.4
  352.6 2.9 copy-start.4
  356.1 2.4 copy-start.5
  366.1 2.9 copy-start.4
  369.6 2.4 copy-start.5
  379.6 2.9 copy-start.4
  383.1 2.4 copy-start.5
  393.0 2.9 copy-start.4
  396.5 2.4 copy-start.5
  406.5 2.9 copy-start.4
  410.0 2.4 copy-start.5
  420.0 2.9 copy-start.4
  423.5 2.4 copy-start.5
  433.5 2.9 copy-start.4
  447.0 2.9 copy-start.4
  460.4 2.9 copy-start.4
  473.9 2.9 copy-start.4
  492.1 10.8 %copy-start.7 = (s32[16,8,4,2]{0,3,2,1:T(2,128)S(1)}, s32[16,8,4,2]{0,3,2,1:T(2,128)}, u32[]{:S(2)}) copy-start(s32[16,8,4,2]{0,3,2,1:T(2,128)} %param.19) | copy-start | bytes 12292
  492.1 11.1 %copy-start.9 = (f32[2048]{0:T(1024)S(1)}, f32[2048]{0:T(1024)}, u32[]{:S(2)}) copy-start(f32[2048]{0:T(1024)} %param.17) | copy-start | bytes 24580
  492.1 11.1 %copy-start.3 = (s32[64,8,128]{2,1,0:T(8,128)S(1)}, s32[64,8,128]{2,1,0:T(8,128)}, u32[]{:S(2)}) copy-start(s32[64,8,128]{2,1,0:T(8,128)} %fusion.43) | copy-start | bytes 786436
  494.5 28.0 %all-to-all-start.1 = ((bf16[8,256,128]{2,0,1:T(8,128)(2,1)}), bf16[8,256,128]{2,0,1:T(8,128)(2,1)S(1)}, u32[]{:S(2)}, u32[]{:S(2)}) async-start(bf16[8,256,128]{2,0,1:T(8,128)(2,1)} %fusion.38), calls=%async_computation.1 | async-start | bytes 1048576 | tf_op jit(solution)/shard_map/all_to_all | solution.py:96
  609.2 4.5 copy-start.8
  609.2 53.1 %all-to-all-start.3 = ((bf16[4,512,512]{2,0,1:T(4,128)(2,1)}), bf16[4,512,512]{2,0,1:T(4,128)(2,1)S(1)}, u32[]{:S(2)}, u32[]{:S(2)}) async-start(bf16[4,512,512]{2,0,1:T(4,128)(2,1)} %copy.189), calls=%async_computation.3 | async-start | bytes 4194304 | tf_op jit(solution)/shard_map/all_to_all | solution.py:136
  669.8 6.0 copy-start.1
  (7 other events, 16.0 us)
